TPU v7x, 128 devices: a whole 4x4x4 slice. The times are simulated.
128 devices in a mesh: pipe: 4 (over y_hi, core), exp: 16 (over x, z), pair: 2 (over y_lo).
Axes of the slice: x: 4, y: 4 (y_hi: 2, y_lo: 2; y = y_hi * 2 + y_lo), z: 4, core: 2. Of those that a mesh axis runs over, the one named last changes fastest.
Arguments:
- hidden_in: bfloat16 [4, 1024, 2048], P(None, ('exp', 'pair')), may hold values from -6 to 6
- routes: int32 [4, 4, 1024, 8], P('pipe', None, ('exp', 'pair')), may hold values from 0 to 63, all different within a row; in each aligned block of 32 rows (0 to 31, 32 to 63, ..., all dimensions but the last counted through in order) at most 6 rows name the same one
- gate_probs: float32 [4, 4, 1024, 8], P('pipe', None, ('exp', 'pair')), may hold values from 0.02 to 1
- norm_gain: float32 [4, 2048], P('pipe'), may hold values from 0.1 to 1.9
- w_gate: bfloat16 [4, 64, 2048, 768], P('pipe', ('exp', 'pair')), may hold values from -0.125 to 0.125
- w_up: bfloat16 [4, 64, 2048, 768], P('pipe', ('exp', 'pair')), may hold values from -0.125 to 0.125
- w_down: bfloat16 [4, 64, 768, 2048], P('pipe', ('exp', 'pair')), may hold values from -0.21875 to 0.21875
Outputs:
- layer_outputs: bfloat16 [4, 4, 1024, 2048], P('pipe', None, ('exp', 'pair'))
Inputs may be any that keep to these rules, and one draw needn't show every extreme that they name: `routes`: within each layer and micro-batch, the 32 tokens of one device (aligned blocks) name no expert more than 6 times in all, and each token names 8 different experts.
All inputs are finite; a program needn't handle non-finite values.
Results may differ from a plain program's by a relative error of at most 0.01.
Values may be sent and summed in bfloat16 or wider, within the bound.
A program may use at most 64 MiB of HBM per device.

v0:
```python
import functools

import jax
import jax.numpy as jnp
from jax import lax
from jax.experimental import pallas as pl
from jax.experimental.pallas import tpu as pltpu
from jax.sharding import PartitionSpec as P

EPS = 1e-06
MESH = pl.DeviceIdType.MESH
F32 = jnp.float32
BF16 = jnp.bfloat16
PIECES = 2
VMEM_LIMIT = 63 * 1024 * 1024


def divisor_tile(size, most):
    tile = most
    while size % tile:
        tile //= 2
    return tile


def relay_kernel(
    stages,
    zs,
    ys,
    pieces,
    hidden_ref,
    routes_ref,
    probs_ref,
    gain_ref,
    wgate_ref,
    wup_ref,
    wdown_ref,
    out_ref,
    wg,
    wu,
    wd,
    hbuf,
    tokens,
    share,
    hid,
    part,
    fromy,
    zsend,
    fromz,
    obuf,
    w_sem,
    h_sem,
    hs_sem,
    o_sem,
    s_sem,
    sr_sem,
    a_sem,
    ar_sem,
    y_sem,
    yr_sem,
    z_sem,
    zr_sem,
):
    micro, rows, width = hbuf.shape
    locals_, _, ff = wg.shape
    lanes = share.shape[3]
    groups = zs * ys
    experts = groups * locals_
    stage = lax.axis_index("pipe")
    z = lax.axis_index("exp")
    y = lax.axis_index("pair")
    me = z * ys + y
    slot = y * zs + z
    upper_half = lax.div(2 * z, zs)
    turn = 1 - 2 * upper_half

    def along(k):
        return lax.rem(z + turn * k + zs, zs)

    def peer(dz, dy):
        return lax.rem(z + dz, zs), lax.rem(y + dy, ys)

    others = [(dz, dy) for dy in range(ys) for dz in range(zs) if dz or dy]

    loads = []
    for j in range(locals_):
        loads.append(
            (
                pltpu.make_async_copy(wgate_ref.at[0, j], wg.at[j], w_sem.at[3 * j]),
                pltpu.make_async_copy(wup_ref.at[0, j], wu.at[j], w_sem.at[3 * j + 1]),
                pltpu.make_async_copy(
                    wdown_ref.at[0, j], wd.at[pl.ds(j * ff, ff)], w_sem.at[3 * j + 2]
                ),
            )
        )

    def from_input(m):
        return pltpu.make_async_copy(hidden_ref.at[m], hbuf.at[m], h_sem.at[m])

    @pl.when(stage == 0)
    def _():
        for m in range(micro):
            from_input(m).start()

    for j in range(locals_):
        loads[j][0].start()
        loads[j][1].start()
    for j in range(locals_):
        loads[j][2].start()

    barrier = pltpu.get_barrier_semaphore()
    for dz, dy in others:
        pz, py = peer(dz, dy)
        pl.semaphore_signal(barrier, inc=1, device_id={"exp": pz, "pair": py}, device_id_type=MESH)

    @pl.when(stage > 0)
    def _():
        pl.semaphore_signal(barrier, inc=1, device_id={"pipe": stage - 1}, device_id_type=MESH)

    @pl.when(stage < stages - 1)
    def _():
        pl.semaphore_signal(barrier, inc=1, device_id={"pipe": stage + 1}, device_id_type=MESH)

    lane = lax.broadcasted_iota(jnp.int32, (rows, lanes), 1)
    for m in range(micro):
        probs = probs_ref[0, m]
        normal = probs / jnp.sum(probs, axis=-1, keepdims=True)
        chosen = routes_ref[0, m]
        total = jnp.zeros((rows, lanes), F32)
        for k in range(chosen.shape[1]):
            named = chosen[:, k : k + 1]
            hit = jnp.logical_or(lane == named, lane == named + experts)
            total = total + jnp.where(hit, normal[:, k : k + 1], 0.0)
        high = total.astype(BF16)
        low = (total - high.astype(F32)).astype(BF16)
        share[slot, m] = jnp.where(lane < experts, high, low)

    linked = (stage > 0).astype(jnp.int32) + (stage < stages - 1).astype(jnp.int32)
    pl.semaphore_wait(barrier, len(others) + linked)

    def share_copy(at, to_z, to_y):
        return pltpu.make_async_remote_copy(
            src_ref=share.at[at],
            dst_ref=share.at[at],
            send_sem=s_sem.at[to_y * zs + to_z],
            recv_sem=sr_sem.at[at],
            device_id={"exp": to_z, "pair": to_y},
            device_id_type=MESH,
        )

    def share_send():
        for dz, dy in others:
            pz, py = peer(dz, dy)
            share_copy(slot, pz, py).start()

    def share_wait():
        for dz, dy in others:
            pz, py = peer(dz, dy)
            share_copy(py * zs + pz, pz, py).wait_recv()

    def token_copy(m, at, tag, to_z, to_y):
        block = tokens.at[m, pl.ds(pl.multiple_of(at * rows, rows), rows)]
        return pltpu.make_async_remote_copy(
            src_ref=block,
            dst_ref=block,
            send_sem=a_sem.at[m, tag],
            recv_sem=ar_sem.at[m, at],
            device_id={"exp": to_z, "pair": to_y},
            device_id_type=MESH,
        )

    def y_copy(m, dy, tz):
        py = lax.rem(y + dy, ys)
        return pltpu.make_async_remote_copy(
            src_ref=part.at[m, pl.ds(pl.multiple_of((py * zs + tz) * rows, rows), rows)],
            dst_ref=fromy.at[m, dy - 1, tz],
            send_sem=y_sem.at[m, dy - 1, tz],
            recv_sem=yr_sem.at[m, dy - 1, tz],
            device_id={"pair": py},
            device_id_type=MESH,
        )

    def z_copy(m, k, source):
        return pltpu.make_async_remote_copy(
            src_ref=zsend.at[m, k],
            dst_ref=fromz.at[m, source],
            send_sem=z_sem.at[m, k - 1],
            recv_sem=zr_sem.at[m, source],
            device_id={"exp": along(k)},
            device_id_type=MESH,
        )

    def hand_copy(m):
        return pltpu.make_async_remote_copy(
            src_ref=obuf.at[m],
            dst_ref=hbuf.at[m],
            send_sem=hs_sem.at[m],
            recv_sem=h_sem.at[m],
            device_id={"pipe": stage + 1},
            device_id_type=MESH,
        )

    def out_copy(m):
        return pltpu.make_async_copy(obuf.at[m], out_ref.at[0, m], o_sem.at[m])

    def announce(m):
        from_input(m).wait()
        state = hbuf[m].astype(F32)
        scale = lax.rsqrt(jnp.mean(state * state, axis=-1, keepdims=True) + EPS)
        tokens[m, pl.ds(pl.multiple_of(slot * rows, rows), rows)] = (
            state * scale * gain_ref[...]
        ).astype(BF16)
        for k in range(zs - 1, 0, -1):
            token_copy(m, slot, k - 1, along(k), y).start()
        for dy in range(1, ys):
            token_copy(m, slot, (zs - 1) + dy - 1, z, lax.rem(y + dy, ys)).start()

    nz = zs - 1

    def forward_tag(dz, dy):
        return nz + (ys - 1) + (dz - 1) * (ys - 1) + dy - 1

    def gather_z(m):
        for dz in range(1, zs):
            pz = along(dz)
            at = y * zs + pz
            token_copy(m, at, dz - 1, pz, y).wait_recv()
            for dy in range(1, ys):
                token_copy(m, at, forward_tag(dz, dy), z, lax.rem(y + dy, ys)).start()

    def gather_y(m, dy):
        py = lax.rem(y + dy, ys)
        for dz in range(zs):
            pz = lax.rem(z + dz, zs)
            token_copy(m, py * zs + pz, 0, z, py).wait_recv()

    ftile = divisor_tile(ff, 256)
    ntile = divisor_tile(width, 512)
    count = groups * rows

    def span(dy):
        return 0, pl.ds(0, count)

    def upper(m, dy):
        at, block = span(dy)
        wide = lax.broadcasted_iota(jnp.int32, (count, lanes), 1)
        shares = share[:, m].reshape(count, lanes).astype(F32)
        for j in range(locals_):
            expert = me * locals_ + j
            mine = jnp.logical_or(wide == expert, wide == expert + experts)
            column = jnp.sum(jnp.where(mine, shares, 0.0), axis=-1, keepdims=True)
            if dy == 0:

                @pl.when(m == 0)
                def _():
                    loads[j][0].wait()
                    loads[j][1].wait()

            for c in range(0, ff, ftile):
                held = tokens[m, block]
                gate = jnp.dot(held, wg[j, :, c : c + ftile], preferred_element_type=F32)
                upward = jnp.dot(held, wu[j, :, c : c + ftile], preferred_element_type=F32)
                hid[block, j * ff + c : j * ff + c + ftile] = (
                    jax.nn.silu(gate) * upward * column
                ).astype(BF16)

    def lower(m, dy):
        _, block = span(dy)
        for c in range(0, width, ntile):
            part[m, block, c : c + ntile] = jnp.dot(
                hid[block], wd[:, c : c + ntile], preferred_element_type=F32
            ).astype(BF16)

    def down_wait(m):
        @pl.when(m == 0)
        def _():
            for j in range(locals_):
                loads[j][2].wait()

    def own_part(m, pz):
        at = pl.multiple_of((y * zs + pz) * rows, rows)
        return part[m, pl.ds(at, rows)].astype(F32)

    def send_y(m, dy):
        for k in range(zs - 1, -1, -1):
            y_copy(m, dy, along(k)).start()

    def scatter(m):
        for k in range(zs - 1, 0, -1):
            pz = along(k)
            total = own_part(m, pz)
            for dy in range(1, ys):
                y_copy(m, dy, pz).wait_recv()
                total = total + fromy[m, dy - 1, pz].astype(F32)
            zsend[m, k] = total.astype(BF16)
            z_copy(m, k, z).start()

    def finish(m):
        total = hbuf[m].astype(F32) + own_part(m, z)
        for dy in range(1, ys):
            y_copy(m, dy, z).wait_recv()
            total = total + fromy[m, dy - 1, z].astype(F32)
        for k in range(1, zs):
            z_copy(m, k, along(k)).wait_recv()
            total = total + fromz[m, along(k)].astype(F32)
        obuf[m] = total.astype(BF16)

        @pl.when(stage < stages - 1)
        def _():
            hand_copy(m).start()

        out_copy(m).start()

    for i in range(pieces):
        announce(i)
    share_send()

    @pl.when(stage == 0)
    def _():
        for i in range(pieces):
            gather_z(i)

    @pl.loop(0, micro // pieces)
    def _(batch):
        m = batch * pieces
        following = m + pieces < micro
        first = jnp.logical_and(stage == 0, following)
        later = jnp.logical_and(stage > 0, following)

        @pl.when(stage > 0)
        def _():
            for i in range(pieces):
                gather_z(m + i)

        @pl.when(first)
        def _():
            for i in range(pieces):
                announce(m + pieces + i)

        @pl.when(m == 0)
        def _():
            share_wait()

        for i in range(pieces):
            for dy in range(1, ys):
                gather_y(m + i, dy)
            upper(m + i, 0)
            if i == 0:
                down_wait(m)
            lower(m + i, 0)
            for dy in range(1, ys):
                send_y(m + i, dy)

        @pl.when(first)
        def _():
            for i in range(pieces):
                gather_z(m + pieces + i)

        for i in range(pieces):
            scatter(m + i)
        for i in range(pieces):
            finish(m + i)

        @pl.when(later)
        def _():
            for i in range(pieces):
                announce(m + pieces + i)

    for dz, dy in others:
        pz, py = peer(dz, dy)
        share_copy(slot, pz, py).wait_send()

    @pl.loop(0, micro)
    def _(m):
        for tag in range(groups - 1):
            token_copy(m, slot, tag, z, y).wait_send()
        for dy in range(1, ys):
            for tz in range(zs):
                y_copy(m, dy, tz).wait_send()
        for dz in range(1, zs):
            z_copy(m, dz, z).wait_send()

        @pl.when(stage < stages - 1)
        def _():
            hand_copy(m).wait_send()

        out_copy(m).wait()


def relayed(hidden_in, routes, gate_probs, norm_gain, w_gate, w_up, w_down):
    batches, whole_rows, _ = hidden_in.shape
    pieces = PIECES if whole_rows % (16 * PIECES) == 0 else 1
    hidden_in = cut(hidden_in, 0, pieces)
    routes = cut(routes, 1, pieces)
    gate_probs = cut(gate_probs, 1, pieces)
    micro, rows, width = hidden_in.shape
    _, locals_, _, ff = w_gate.shape
    stages, zs, ys = (lax.axis_size(a) for a in ("pipe", "exp", "pair"))
    groups = zs * ys
    lanes = share_lanes(groups * locals_)
    dma = pltpu.SemaphoreType.DMA
    anywhere = pl.BlockSpec(memory_space=pl.ANY)
    inside = pl.BlockSpec(memory_space=pltpu.VMEM)
    out = pl.pallas_call(
        functools.partial(relay_kernel, stages, zs, ys, pieces),
        out_shape=jax.ShapeDtypeStruct((1, micro, rows, width), BF16),
        in_specs=[anywhere, inside, inside, inside, anywhere, anywhere, anywhere],
        out_specs=anywhere,
        scratch_shapes=[
            pltpu.VMEM((locals_, width, ff), BF16),
            pltpu.VMEM((locals_, width, ff), BF16),
            pltpu.VMEM((locals_ * ff, width), BF16),
            pltpu.VMEM((micro, rows, width), BF16),
            pltpu.VMEM((micro, groups * rows, width), BF16),
            pltpu.VMEM((groups, micro, rows, lanes), BF16),
            pltpu.VMEM((groups * rows, locals_ * ff), BF16),
            pltpu.VMEM((micro, groups * rows, width), BF16),
            pltpu.VMEM((micro, max(1, ys - 1), zs, rows, width), BF16),
            pltpu.VMEM((micro, zs, rows, width), BF16),
            pltpu.VMEM((micro, zs, rows, width), BF16),
            pltpu.VMEM((micro, rows, width), BF16),
            dma((3 * locals_,)),
            dma((micro,)),
            dma((micro,)),
            dma((micro,)),
            dma((groups,)),
            dma((groups,)),
            dma((micro, groups)),
            dma((micro, groups)),
            dma((micro, max(1, ys - 1), zs)),
            dma((micro, max(1, ys - 1), zs)),
            dma((micro, max(1, zs - 1))),
            dma((micro, zs)),
        ],
        compiler_params=pltpu.CompilerParams(
            collective_id=0, has_side_effects=True, vmem_limit_bytes=VMEM_LIMIT
        ),
    )(hidden_in, routes, gate_probs, norm_gain, w_gate, w_up, w_down)
    return out.reshape(1, batches, whole_rows, width)


def cut(value, axis, pieces):
    shape = value.shape
    rows = shape[axis + 1] // pieces
    return value.reshape(shape[:axis] + (shape[axis] * pieces, rows) + shape[axis + 2 :])


def share_lanes(experts):
    return -(-2 * experts // 128) * 128


def kernel_fits(hidden_in, w_gate, groups):
    micro, rows, width = hidden_in.shape
    _, locals_, _, ff = w_gate.shape
    weights = 3 * locals_ * width * ff
    moved = micro * rows * width * (4 * groups + 5)
    small = groups * rows * (locals_ * ff + micro * share_lanes(groups * locals_))
    fits = 2 * (weights + moved + small) + 8 * 1024 * 1024 < VMEM_LIMIT
    return fits and rows % 16 == 0 and width % 128 == 0 and ff % 128 == 0


def passed_along(value, axis, steps):
    count = lax.axis_size(axis)
    first, last = (max(0, -steps), min(count, count - steps))
    return lax.ppermute(value, axis, [(source, source + steps) for source in range(first, last)])


def expert_block(arrived, wgate, wupper, wdown):
    gate = jnp.einsum("nlcd,ldf->nlcf", arrived, wgate, preferred_element_type=jnp.float32)
    upward = jnp.einsum("nlcd,ldf->nlcf", arrived, wupper, preferred_element_type=jnp.float32)
    hidden = (jax.nn.silu(gate) * upward).astype(jnp.bfloat16)
    return jnp.einsum("nlcf,lfd->nlcd", hidden, wdown, preferred_element_type=jnp.float32).astype(
        jnp.bfloat16
    )


def on_device(hidden_in, routes, gate_probs, norm_gain, w_gate, w_up, w_down):
    if kernel_fits(hidden_in, w_gate, lax.axis_size(("exp", "pair"))):
        return relayed(hidden_in, routes, gate_probs, norm_gain, w_gate, w_up, w_down)
    section = lax.axis_index("pipe")
    micro, tok_rows, width = hidden_in.shape
    top_count = routes.shape[3]
    groups = lax.axis_size(("exp", "pair"))
    local_experts = w_gate.shape[1]
    experts = local_experts * groups
    capacity = max(2, 3 * tok_rows * top_count // (2 * experts))
    gain = norm_gain[0]
    wgate = w_gate[0]
    wupper = w_up[0]
    wdown = w_down[0]
    expert_ids = jnp.arange(experts, dtype=jnp.int32)

    def layer(state, index):
        chosen = lax.dynamic_index_in_dim(routes[0], index, 0, keepdims=False).reshape(-1)
        probs = lax.dynamic_index_in_dim(gate_probs[0], index, 0, keepdims=False)
        floated = state.astype(jnp.float32)
        scale = lax.rsqrt(jnp.mean(floated * floated, axis=-1, keepdims=True) + EPS)
        normed = (floated * scale * gain).astype(jnp.bfloat16)
        onehot = (chosen[:, None] == expert_ids[None, :]).astype(jnp.int32)
        before = jnp.cumsum(onehot, axis=0) - onehot
        slots = jnp.sum(before * onehot, axis=1)
        outgoing = jnp.zeros((experts, capacity, width), jnp.bfloat16)
        outgoing = outgoing.at[chosen, slots].set(jnp.repeat(normed, top_count, axis=0))
        grouped = outgoing.reshape(groups, local_experts, capacity, width)
        produced = expert_block(
            lax.all_to_all(grouped, ("exp", "pair"), split_axis=0, concat_axis=0, tiled=True),
            wgate,
            wupper,
            wdown,
        )
        returned = lax.all_to_all(
            produced, ("exp", "pair"), split_axis=0, concat_axis=0, tiled=True
        )
        results = returned.reshape(experts, capacity, width)[chosen, slots]
        results = results.reshape(tok_rows, top_count, width).astype(jnp.float32)
        weights = probs / jnp.sum(probs, axis=-1, keepdims=True)
        mixed = jnp.einsum("tk,tkd->td", weights, results)
        return (floated + mixed).astype(jnp.bfloat16)

    def advance(step, carry):
        received, saved = carry
        index = step - section
        valid = jnp.logical_and(index >= 0, index < micro)
        clipped = jnp.clip(index, 0, micro - 1)
        first = lax.dynamic_index_in_dim(hidden_in, clipped, 0, keepdims=False)
        state = jnp.where(section == 0, first, received)
        updated = layer(state, clipped)
        saved = jnp.where(valid, lax.dynamic_update_index_in_dim(saved, updated, clipped, 0), saved)
        received = passed_along(updated, "pipe", 1)
        return (received, saved)

    start = (
        jnp.zeros((tok_rows, width), jnp.bfloat16),
        jnp.zeros((micro, tok_rows, width), jnp.bfloat16),
    )
    received, saved = lax.fori_loop(0, micro + lax.axis_size("pipe") - 1, advance, start)
    return saved[None]


def solution(mesh):
    in_specs = (
        P(None, ("exp", "pair"), None),
        P("pipe", None, ("exp", "pair"), None),
        P("pipe", None, ("exp", "pair"), None),
        P("pipe", None),
        P("pipe", ("exp", "pair"), None, None),
        P("pipe", ("exp", "pair"), None, None),
        P("pipe", ("exp", "pair"), None, None),
    )
    out_specs = P("pipe", None, ("exp", "pair"), None)
    return jax.shard_map(
        on_device, mesh=mesh, in_specs=in_specs, out_specs=out_specs, check_vma=False
    )
```

profile of v0, /device:TPU:1, one launch (start us, length us, event | category | flops | bytes accessed | tf_op | source)
XLA Modules:
  0.0 810.7 jit_solution(4806493436090635416)
XLA Ops:
  0.9 809.8 %while.18 = (s32[]{:T(128)}, bf16[32,2048]{1,0:T(8,128)(2,1)S(1)}, bf16[4,32,2048]{2,1,0:T(8,128)(2,1)}, pred[]{:T(512)}, s32[]{:T(128)}, /*index=5*/bf16[4,32,2...) while((s32[]{:T(128)}, bf16[32,2048]{1,0:T(8,128)(2,1)S(1)}, ...), condition=%wide.region_7.8_spmd.clone.clone, body=%wide.region_0.7_spmd.clone.clone.sunk | while | flops 3630486016 | bytes 61134680 | solution.py:535
  5.1 22.3 %scatter_fusion = bf16[64,6,2048]{2,0,1:T(8,128)(2,1)S(1)} fusion(bf16[64,6,2048]{2,0,1:T(8,128)(2,1)S(1)} %broadcast.267, s32[256]{0:T(256)S(1)} %bitcast.139, bf16[256,2048]{1,0:T(8,128)(2,1)S(1)} %broadcast_bitcast_fusion.2), kind=kCustom, calls=%fused_computation.1.clone.clone.1 | custom fusion | bytes 3147776 | tf_op jit(solution)/shard_map/while/body/eval_jaxpr/scatter | solution.py:502
  30.2 31.7 %all_to_all.26 = bf16[32,2,6,2048]{3,1,2,0:T(2,128)(2,1)S(1)} all-to-all(bf16[32,2,6,2048]{3,1,2,0:T(2,128)(2,1)S(1)} %copy.58), channel_id=1, replica_groups=mesh['pipe'=4,'exp'=16,'pair'=2] {'exp','pair'}, dimensions={0} | all-to-all | bytes 3145728 | tf_op jit(solution)/shard_map/while/body/eval_jaxpr/all_to_all | solution.py:505
  61.8 6.4 fusion.86
  68.2 8.9 %fusion.87 = bf16[32,2,6,2048]{3,0,2,1:T(8,128)(2,1)S(1)} fusion(bf16[2,768,2048]{2,1,0:T(8,128)(2,1)} %get-tuple-element.525, bf16[2,2048,768]{2,1,0:T(8,128)(2,1)} %get-tuple-element.524, bf16[32,2,6,2048]{3,1,2,0:T(2,128)(2,1)S(1)} %all_to_all.26, f32[32,2,6,768]{3,0,2,1:T(8,128)} %fusion.86), kind=kOutput, calls=%fused_computation.10.clone.1 | convolution fusion | flops 2418475008 | bytes 16908288 | tf_op jit(solution)/shard_map/while/body/eval_jaxpr/nlcf,lfd->nlcd/dot_general | solution.py:471
  77.1 2.8 copy.59
  79.9 4.5 all-to-all-start.1
  84.6 20.8 %all-to-all-done.1 = bf16[32,2,6,2048]{3,1,2,0:T(2,128)(2,1)S(1)} async-done(((bf16[32,2,6,2048]{3,1,2,0:T(2,128)(2,1)}), bf16[32,2,6,2048]{3,1,2,0:T(2,128)(2,1)S(1)}, u32[]{:S(2)}, u32[]{:S(2)}) %all-to-all-start.1) | async-done | bytes 1572896 | tf_op jit(solution)/shard_map/while/body/eval_jaxpr/all_to_all | solution.py:510
  107.2 4.3 gather_fusion
  113.6 7.4 collective-permute-start
  121.0 1.9 collective-permute-done
  127.1 22.3 %scatter_fusion = bf16[64,6,2048]{2,0,1:T(8,128)(2,1)S(1)} fusion(bf16[64,6,2048]{2,0,1:T(8,128)(2,1)S(1)} %broadcast.267, s32[256]{0:T(256)S(1)} %bitcast.139, bf16[256,2048]{1,0:T(8,128)(2,1)S(1)} %broadcast_bitcast_fusion.2), kind=kCustom, calls=%fused_computation.1.clone.clone.1 | custom fusion | bytes 3147776 | tf_op jit(solution)/shard_map/while/body/eval_jaxpr/scatter | solution.py:502
  152.2 25.0 %all_to_all.26 = bf16[32,2,6,2048]{3,1,2,0:T(2,128)(2,1)S(1)} all-to-all(bf16[32,2,6,2048]{3,1,2,0:T(2,128)(2,1)S(1)} %copy.58), channel_id=1, replica_groups=mesh['pipe'=4,'exp'=16,'pair'=2] {'exp','pair'}, dimensions={0} | all-to-all | bytes 3145728 | tf_op jit(solution)/shard_map/while/body/eval_jaxpr/all_to_all | solution.py:505
  177.1 6.4 fusion.86
  183.6 8.9 %fusion.87 = bf16[32,2,6,2048]{3,0,2,1:T(8,128)(2,1)S(1)} fusion(bf16[2,768,2048]{2,1,0:T(8,128)(2,1)} %get-tuple-element.525, bf16[2,2048,768]{2,1,0:T(8,128)(2,1)} %get-tuple-element.524, bf16[32,2,6,2048]{3,1,2,0:T(2,128)(2,1)S(1)} %all_to_all.26, f32[32,2,6,768]{3,0,2,1:T(8,128)} %fusion.86), kind=kOutput, calls=%fused_computation.10.clone.1 | convolution fusion | flops 2418475008 | bytes 16908288 | tf_op jit(solution)/shard_map/while/body/eval_jaxpr/nlcf,lfd->nlcd/dot_general | solution.py:471
  192.5 2.8 copy.59
  195.2 4.1 all-to-all-start.1
  199.5 22.3 %all-to-all-done.1 = bf16[32,2,6,2048]{3,1,2,0:T(2,128)(2,1)S(1)} async-done(((bf16[32,2,6,2048]{3,1,2,0:T(2,128)(2,1)}), bf16[32,2,6,2048]{3,1,2,0:T(2,128)(2,1)S(1)}, u32[]{:S(2)}, u32[]{:S(2)}) %all-to-all-start.1) | async-done | bytes 1572896 | tf_op jit(solution)/shard_map/while/body/eval_jaxpr/all_to_all | solution.py:510
  223.6 4.3 gather_fusion
  231.9 1.9 collective-permute-done
  238.1 22.3 %scatter_fusion = bf16[64,6,2048]{2,0,1:T(8,128)(2,1)S(1)} fusion(bf16[64,6,2048]{2,0,1:T(8,128)(2,1)S(1)} %broadcast.267, s32[256]{0:T(256)S(1)} %bitcast.139, bf16[256,2048]{1,0:T(8,128)(2,1)S(1)} %broadcast_bitcast_fusion.2), kind=kCustom, calls=%fused_computation.1.clone.clone.1 | custom fusion | bytes 3147776 | tf_op jit(solution)/shard_map/while/body/eval_jaxpr/scatter | solution.py:502
  263.1 28.1 %all_to_all.26 = bf16[32,2,6,2048]{3,1,2,0:T(2,128)(2,1)S(1)} all-to-all(bf16[32,2,6,2048]{3,1,2,0:T(2,128)(2,1)S(1)} %copy.58), channel_id=1, replica_groups=mesh['pipe'=4,'exp'=16,'pair'=2] {'exp','pair'}, dimensions={0} | all-to-all | bytes 3145728 | tf_op jit(solution)/shard_map/while/body/eval_jaxpr/all_to_all | solution.py:505
  291.2 6.4 fusion.86
  297.7 8.9 %fusion.87 = bf16[32,2,6,2048]{3,0,2,1:T(8,128)(2,1)S(1)} fusion(bf16[2,768,2048]{2,1,0:T(8,128)(2,1)} %get-tuple-element.525, bf16[2,2048,768]{2,1,0:T(8,128)(2,1)} %get-tuple-element.524, bf16[32,2,6,2048]{3,1,2,0:T(2,128)(2,1)S(1)} %all_to_all.26, f32[32,2,6,768]{3,0,2,1:T(8,128)} %fusion.86), kind=kOutput, calls=%fused_computation.10.clone.1 | convolution fusion | flops 2418475008 | bytes 16908288 | tf_op jit(solution)/shard_map/while/body/eval_jaxpr/nlcf,lfd->nlcd/dot_general | solution.py:471
  306.6 2.8 copy.59
  309.4 4.8 all-to-all-start.1
  314.3 22.2 %all-to-all-done.1 = bf16[32,2,6,2048]{3,1,2,0:T(2,128)(2,1)S(1)} async-done(((bf16[32,2,6,2048]{3,1,2,0:T(2,128)(2,1)}), bf16[32,2,6,2048]{3,1,2,0:T(2,128)(2,1)S(1)}, u32[]{:S(2)}, u32[]{:S(2)}) %all-to-all-start.1) | async-done | bytes 1572896 | tf_op jit(solution)/shard_map/while/body/eval_jaxpr/all_to_all | solution.py:510
  338.3 4.3 gather_fusion
  346.7 1.9 collective-permute-done
  352.9 22.3 %scatter_fusion = bf16[64,6,2048]{2,0,1:T(8,128)(2,1)S(1)} fusion(bf16[64,6,2048]{2,0,1:T(8,128)(2,1)S(1)} %broadcast.267, s32[256]{0:T(256)S(1)} %bitcast.139, bf16[256,2048]{1,0:T(8,128)(2,1)S(1)} %broadcast_bitcast_fusion.2), kind=kCustom, calls=%fused_computation.1.clone.clone.1 | custom fusion | bytes 3147776 | tf_op jit(solution)/shard_map/while/body/eval_jaxpr/scatter | solution.py:502
  377.9 29.0 %all_to_all.26 = bf16[32,2,6,2048]{3,1,2,0:T(2,128)(2,1)S(1)} all-to-all(bf16[32,2,6,2048]{3,1,2,0:T(2,128)(2,1)S(1)} %copy.58), channel_id=1, replica_groups=mesh['pipe'=4,'exp'=16,'pair'=2] {'exp','pair'}, dimensions={0} | all-to-all | bytes 3145728 | tf_op jit(solution)/shard_map/while/body/eval_jaxpr/all_to_all | solution.py:505
  406.8 6.4 fusion.86
  413.3 8.9 %fusion.87 = bf16[32,2,6,2048]{3,0,2,1:T(8,128)(2,1)S(1)} fusion(bf16[2,768,2048]{2,1,0:T(8,128)(2,1)} %get-tuple-element.525, bf16[2,2048,768]{2,1,0:T(8,128)(2,1)} %get-tuple-element.524, bf16[32,2,6,2048]{3,1,2,0:T(2,128)(2,1)S(1)} %all_to_all.26, f32[32,2,6,768]{3,0,2,1:T(8,128)} %fusion.86), kind=kOutput, calls=%fused_computation.10.clone.1 | convolution fusion | flops 2418475008 | bytes 16908288 | tf_op jit(solution)/shard_map/while/body/eval_jaxpr/nlcf,lfd->nlcd/dot_general | solution.py:471
  422.2 2.8 copy.59
  425.0 4.7 all-to-all-start.1
  429.9 22.2 %all-to-all-done.1 = bf16[32,2,6,2048]{3,1,2,0:T(2,128)(2,1)S(1)} async-done(((bf16[32,2,6,2048]{3,1,2,0:T(2,128)(2,1)}), bf16[32,2,6,2048]{3,1,2,0:T(2,128)(2,1)S(1)}, u32[]{:S(2)}, u32[]{:S(2)}) %all-to-all-start.1) | async-done | bytes 1572896 | tf_op jit(solution)/shard_map/while/body/eval_jaxpr/all_to_all | solution.py:510
  453.9 4.3 gather_fusion
  462.3 1.9 collective-permute-done
  468.4 22.3 %scatter_fusion = bf16[64,6,2048]{2,0,1:T(8,128)(2,1)S(1)} fusion(bf16[64,6,2048]{2,0,1:T(8,128)(2,1)S(1)} %broadcast.267, s32[256]{0:T(256)S(1)} %bitcast.139, bf16[256,2048]{1,0:T(8,128)(2,1)S(1)} %broadcast_bitcast_fusion.2), kind=kCustom, calls=%fused_computation.1.clone.clone.1 | custom fusion | bytes 3147776 | tf_op jit(solution)/shard_map/while/body/eval_jaxpr/scatter | solution.py:502
  493.4 28.9 %all_to_all.26 = bf16[32,2,6,2048]{3,1,2,0:T(2,128)(2,1)S(1)} all-to-all(bf16[32,2,6,2048]{3,1,2,0:T(2,128)(2,1)S(1)} %copy.58), channel_id=1, replica_groups=mesh['pipe'=4,'exp'=16,'pair'=2] {'exp','pair'}, dimensions={0} | all-to-all | bytes 3145728 | tf_op jit(solution)/shard_map/while/body/eval_jaxpr/all_to_all | solution.py:505
  522.4 6.4 fusion.86
  528.8 8.9 %fusion.87 = bf16[32,2,6,2048]{3,0,2,1:T(8,128)(2,1)S(1)} fusion(bf16[2,768,2048]{2,1,0:T(8,128)(2,1)} %get-tuple-element.525, bf16[2,2048,768]{2,1,0:T(8,128)(2,1)} %get-tuple-element.524, bf16[32,2,6,2048]{3,1,2,0:T(2,128)(2,1)S(1)} %all_to_all.26, f32[32,2,6,768]{3,0,2,1:T(8,128)} %fusion.86), kind=kOutput, calls=%fused_computation.10.clone.1 | convolution fusion | flops 2418475008 | bytes 16908288 | tf_op jit(solution)/shard_map/while/body/eval_jaxpr/nlcf,lfd->nlcd/dot_general | solution.py:471
  537.7 2.8 copy.59
  540.5 4.8 all-to-all-start.1
  545.4 22.2 %all-to-all-done.1 = bf16[32,2,6,2048]{3,1,2,0:T(2,128)(2,1)S(1)} async-done(((bf16[32,2,6,2048]{3,1,2,0:T(2,128)(2,1)}), bf16[32,2,6,2048]{3,1,2,0:T(2,128)(2,1)S(1)}, u32[]{:S(2)}, u32[]{:S(2)}) %all-to-all-start.1) | async-done | bytes 1572896 | tf_op jit(solution)/shard_map/while/body/eval_jaxpr/all_to_all | solution.py:510
  569.5 4.3 gather_fusion
  577.8 1.9 collective-permute-done
  584.0 22.3 %scatter_fusion = bf16[64,6,2048]{2,0,1:T(8,128)(2,1)S(1)} fusion(bf16[64,6,2048]{2,0,1:T(8,128)(2,1)S(1)} %broadcast.267, s32[256]{0:T(256)S(1)} %bitcast.139, bf16[256,2048]{1,0:T(8,128)(2,1)S(1)} %broadcast_bitcast_fusion.2), kind=kCustom, calls=%fused_computation.1.clone.clone.1 | custom fusion | bytes 3147776 | tf_op jit(solution)/shard_map/while/body/eval_jaxpr/scatter | solution.py:502
  609.0 28.9 %all_to_all.26 = bf16[32,2,6,2048]{3,1,2,0:T(2,128)(2,1)S(1)} all-to-all(bf16[32,2,6,2048]{3,1,2,0:T(2,128)(2,1)S(1)} %copy.58), channel_id=1, replica_groups=mesh['pipe'=4,'exp'=16,'pair'=2] {'exp','pair'}, dimensions={0} | all-to-all | bytes 3145728 | tf_op jit(solution)/shard_map/while/body/eval_jaxpr/all_to_all | solution.py:505
  637.9 6.4 fusion.86
  644.3 8.9 %fusion.87 = bf16[32,2,6,2048]{3,0,2,1:T(8,128)(2,1)S(1)} fusion(bf16[2,768,2048]{2,1,0:T(8,128)(2,1)} %get-tuple-element.525, bf16[2,2048,768]{2,1,0:T(8,128)(2,1)} %get-tuple-element.524, bf16[32,2,6,2048]{3,1,2,0:T(2,128)(2,1)S(1)} %all_to_all.26, f32[32,2,6,768]{3,0,2,1:T(8,128)} %fusion.86), kind=kOutput, calls=%fused_computation.10.clone.1 | convolution fusion | flops 2418475008 | bytes 16908288 | tf_op jit(solution)/shard_map/while/body/eval_jaxpr/nlcf,lfd->nlcd/dot_general | solution.py:471
  653.2 2.8 copy.59
  656.0 4.8 all-to-all-start.1
  660.9 22.2 %all-to-all-done.1 = bf16[32,2,6,2048]{3,1,2,0:T(2,128)(2,1)S(1)} async-done(((bf16[32,2,6,2048]{3,1,2,0:T(2,128)(2,1)}), bf16[32,2,6,2048]{3,1,2,0:T(2,128)(2,1)S(1)}, u32[]{:S(2)}, u32[]{:S(2)}) %all-to-all-start.1) | async-done | bytes 1572896 | tf_op jit(solution)/shard_map/while/body/eval_jaxpr/all_to_all | solution.py:510
  685.0 4.3 gather_fusion
  699.5 22.3 %scatter_fusion = bf16[64,6,2048]{2,0,1:T(8,128)(2,1)S(1)} fusion(bf16[64,6,2048]{2,0,1:T(8,128)(2,1)S(1)} %broadcast.267, s32[256]{0:T(256)S(1)} %bitcast.139, bf16[256,2048]{1,0:T(8,128)(2,1)S(1)} %broadcast_bitcast_fusion.2), kind=kCustom, calls=%fused_computation.1.clone.clone.1 | custom fusion | bytes 3147776 | tf_op jit(solution)/shard_map/while/body/eval_jaxpr/scatter | solution.py:502
  724.5 28.9 %all_to_all.26 = bf16[32,2,6,2048]{3,1,2,0:T(2,128)(2,1)S(1)} all-to-all(bf16[32,2,6,2048]{3,1,2,0:T(2,128)(2,1)S(1)} %copy.58), channel_id=1, replica_groups=mesh['pipe'=4,'exp'=16,'pair'=2] {'exp','pair'}, dimensions={0} | all-to-all | bytes 3145728 | tf_op jit(solution)/shard_map/while/body/eval_jaxpr/all_to_all | solution.py:505
  753.4 6.4 fusion.86
  759.8 8.9 %fusion.87 = bf16[32,2,6,2048]{3,0,2,1:T(8,128)(2,1)S(1)} fusion(bf16[2,768,2048]{2,1,0:T(8,128)(2,1)} %get-tuple-element.525, bf16[2,2048,768]{2,1,0:T(8,128)(2,1)} %get-tuple-element.524, bf16[32,2,6,2048]{3,1,2,0:T(2,128)(2,1)S(1)} %all_to_all.26, f32[32,2,6,768]{3,0,2,1:T(8,128)} %fusion.86), kind=kOutput, calls=%fused_computation.10.clone.1 | convolution fusion | flops 2418475008 | bytes 16908288 | tf_op jit(solution)/shard_map/while/body/eval_jaxpr/nlcf,lfd->nlcd/dot_general | solution.py:471
  768.7 2.8 copy.59
  771.5 4.8 all-to-all-start.1
  776.4 22.2 %all-to-all-done.1 = bf16[32,2,6,2048]{3,1,2,0:T(2,128)(2,1)S(1)} async-done(((bf16[32,2,6,2048]{3,1,2,0:T(2,128)(2,1)}), bf16[32,2,6,2048]{3,1,2,0:T(2,128)(2,1)S(1)}, u32[]{:S(2)}, u32[]{:S(2)}) %all-to-all-start.1) | async-done | bytes 1572896 | tf_op jit(solution)/shard_map/while/body/eval_jaxpr/all_to_all | solution.py:510
  800.4 4.3 gather_fusion
  808.8 1.9 collective-permute-done
  (205 shorter events, 90.6 us)
Async XLA Ops:
  79.9 4.5 copy-start
  79.9 25.5 %all-to-all-start.1 = ((bf16[32,2,6,2048]{3,1,2,0:T(2,128)(2,1)}), bf16[32,2,6,2048]{3,1,2,0:T(2,128)(2,1)S(1)}, u32[]{:S(2)}, u32[]{:S(2)}) async-start(bf16[32,2,6,2048]{3,1,2,0:T(2,128)(2,1)} %copy.59), calls=%async_computation.1 | async-start | bytes 3145728 | tf_op jit(solution)/shard_map/while/body/eval_jaxpr/all_to_all | solution.py:510
  113.6 9.3 %collective-permute-start = (bf16[32,2048]{1,0:T(8,128)(2,1)S(1)}, bf16[32,2048]{1,0:T(8,128)(2,1)S(1)}, u32[]{:S(2)}, u32[]{:S(2)}) collective-permute-start(bf16[32,2048]{1,0:T(8,128)(2,1)S(1)} %get-tuple-element.478), channel_id=1, source_target_pairs={{0,32},{32,64},{64,96},{1,33},{33,65},{65,97},{2,34},{34,66},{66,9... | collective-permute-start | bytes 393224 | tf_op jit(solution)/shard_map/while/body/eval_jaxpr/ppermute | solution.py:464
  195.2 4.1 copy-start
  195.2 26.5 %all-to-all-start.1 = ((bf16[32,2,6,2048]{3,1,2,0:T(2,128)(2,1)}), bf16[32,2,6,2048]{3,1,2,0:T(2,128)(2,1)S(1)}, u32[]{:S(2)}, u32[]{:S(2)}) async-start(bf16[32,2,6,2048]{3,1,2,0:T(2,128)(2,1)} %copy.59), calls=%async_computation.1 | async-start | bytes 3145728 | tf_op jit(solution)/shard_map/while/body/eval_jaxpr/all_to_all | solution.py:510
  230.0 3.8 collective-permute-start
  309.3 4.8 copy-start
  309.4 27.2 %all-to-all-start.1 = ((bf16[32,2,6,2048]{3,1,2,0:T(2,128)(2,1)}), bf16[32,2,6,2048]{3,1,2,0:T(2,128)(2,1)S(1)}, u32[]{:S(2)}, u32[]{:S(2)}) async-start(bf16[32,2,6,2048]{3,1,2,0:T(2,128)(2,1)} %copy.59), calls=%async_computation.1 | async-start | bytes 3145728 | tf_op jit(solution)/shard_map/while/body/eval_jaxpr/all_to_all | solution.py:510
  344.8 3.8 collective-permute-start
  424.9 4.8 copy-start
  425.0 27.2 %all-to-all-start.1 = ((bf16[32,2,6,2048]{3,1,2,0:T(2,128)(2,1)}), bf16[32,2,6,2048]{3,1,2,0:T(2,128)(2,1)S(1)}, u32[]{:S(2)}, u32[]{:S(2)}) async-start(bf16[32,2,6,2048]{3,1,2,0:T(2,128)(2,1)} %copy.59), calls=%async_computation.1 | async-start | bytes 3145728 | tf_op jit(solution)/shard_map/while/body/eval_jaxpr/all_to_all | solution.py:510
  460.3 3.8 collective-permute-start
  540.5 4.8 copy-start
  540.5 27.2 %all-to-all-start.1 = ((bf16[32,2,6,2048]{3,1,2,0:T(2,128)(2,1)}), bf16[32,2,6,2048]{3,1,2,0:T(2,128)(2,1)S(1)}, u32[]{:S(2)}, u32[]{:S(2)}) async-start(bf16[32,2,6,2048]{3,1,2,0:T(2,128)(2,1)} %copy.59), calls=%async_computation.1 | async-start | bytes 3145728 | tf_op jit(solution)/shard_map/while/body/eval_jaxpr/all_to_all | solution.py:510
  575.9 3.8 collective-permute-start
  656.0 4.8 copy-start
  656.0 27.2 %all-to-all-start.1 = ((bf16[32,2,6,2048]{3,1,2,0:T(2,128)(2,1)}), bf16[32,2,6,2048]{3,1,2,0:T(2,128)(2,1)S(1)}, u32[]{:S(2)}, u32[]{:S(2)}) async-start(bf16[32,2,6,2048]{3,1,2,0:T(2,128)(2,1)} %copy.59), calls=%async_computation.1 | async-start | bytes 3145728 | tf_op jit(solution)/shard_map/while/body/eval_jaxpr/all_to_all | solution.py:510
  691.4 3.8 collective-permute-start
  771.5 4.8 copy-start
  771.5 27.2 %all-to-all-start.1 = ((bf16[32,2,6,2048]{3,1,2,0:T(2,128)(2,1)}), bf16[32,2,6,2048]{3,1,2,0:T(2,128)(2,1)S(1)}, u32[]{:S(2)}, u32[]{:S(2)}) async-start(bf16[32,2,6,2048]{3,1,2,0:T(2,128)(2,1)} %copy.59), calls=%async_computation.1 | async-start | bytes 3145728 | tf_op jit(solution)/shard_map/while/body/eval_jaxpr/all_to_all | solution.py:510
  806.9 3.8 collective-permute-start
where the time goes:
time: 813 us; the launch traced here: 811 us
  local copies, waits for them, and re-layouts  250 us (31%)
  blocking collectives  200 us (25%)
  waiting for transfers between devices  168 us (21%)
  matrix products  110 us (14%)
  starting transfers between devices  51.2 us (6%)
  other arithmetic  30.6 us (4%)
    all_to_all x7, blocking collectives, layer(): lax.all_to_all(grouped, ('exp', 'pair'), split_axis=0, concat_axis=0, til...  200 us
    scatter x7, local copies, waits for them, and re-layouts, layer(): outgoing.at[chosen, slots].set(jnp.repeat(normed, top_count, axis=0))  156 us
    all_to_all x7, waiting for transfers between devices, layer(): lax.all_to_all(produced, ('exp', 'pair'), split_axis=0, concat_axis=0, ti...  154 us
    dot_general x7, matrix products, expert_block(): jnp.einsum('nlcf,lfd->nlcd', hidden, wdown, preferred_element_type=jnp.fl...  62.2 us
    dot_general x7, matrix products, expert_block(): jnp.einsum('nlcd,ldf->nlcf', arrived, wgate, preferred_element_type=jnp.f...  45 us
    all_to_all x7, starting transfers between devices, layer(): lax.all_to_all(produced, ('exp', 'pair'), split_axis=0, concat_axis=0, ti...  32.4 us
    gather x7, local copies, waits for them, and re-layouts, layer(): results = returned.reshape(experts, capacity, width)[chosen, slots]  30.1 us
    convert_element_type x7, local copies, waits for them, and re-layouts, expert_block(): jnp.einsum('nlcf,lfd->nlcd', hidden, wdown, preferred_element_type=jnp.fl...  19.5 us
  transfers between devices with their start and end apart: 14, of which 14 were waited for; matrix products, arithmetic and copies ran while one was open for 0% of the time, Pallas kernels for 0%

commit v1 on v0

v1 whole, which is shorter than its diff:
```python
import functools

import jax
import jax.numpy as jnp
from jax import lax
from jax.experimental import pallas as pl
from jax.experimental.pallas import tpu as pltpu
from jax.sharding import PartitionSpec as P

EPS = 1e-06
MESH = pl.DeviceIdType.MESH
F32 = jnp.float32
BF16 = jnp.bfloat16
VMEM_LIMIT = 63 * 1024 * 1024
SLOTS = 6
SIDE = 4
QUARTERS = 4
CHUNKS = 2
LANES = 128
UNITS = 8


def fdiv(value, n):
    return jnp.floor((value + 0.5) * (1.0 / n))


def iota(shape, axis):
    return lax.broadcasted_iota(jnp.int32, shape, axis).astype(F32)


def dot(a, b):
    return jnp.dot(a, b, preferred_element_type=F32)


def dot_nt(a, b):
    return lax.dot_general(a, b, (((1,), (1,)), ((), ())), preferred_element_type=F32)


def relay_kernel(
    stages,
    zs,
    ys,
    hidden_ref,
    routes_ref,
    probs_ref,
    gain_ref,
    wgate_ref,
    wup_ref,
    wdown_ref,
    out_ref,
    wg,
    wu,
    wd,
    hbuf,
    obuf,
    xq,
    sendbuf,
    recvbuf,
    backbuf,
    homebuf,
    xe,
    acc,
    hid,
    stack,
    sel,
    pick_g,
    pick_s,
    gath,
    comb,
    unpack,
    repack,
    w_sem,
    h_sem,
    hs_sem,
    o_sem,
    a_sem,
    ar_sem,
    b_sem,
    br_sem,
):
    micro, rows, width = hbuf.shape
    locals_, _, ff = wg.shape
    groups = zs * ys
    block = QUARTERS * locals_ * SLOTS
    total = groups * block
    half = locals_ * SLOTS
    cw = width // CHUNKS
    qw = cw // QUARTERS
    unit = UNITS * block
    units = groups // UNITS
    per = UNITS * SLOTS
    erows = groups * SLOTS

    stage = lax.axis_index("pipe")
    e_idx = lax.axis_index("exp")
    y = lax.axis_index("pair")
    me = e_idx * ys + y
    cx = lax.div(e_idx, SIDE)
    cz = lax.rem(e_idx, SIDE)

    def ring(d):
        return min(d, SIDE - d)

    offsets = [
        (dx, dz, dy)
        for dx in range(zs // SIDE)
        for dz in range(SIDE)
        for dy in range(ys)
        if dx or dz or dy
    ]
    offsets.sort(key=lambda o: -(ring(o[0]) + ring(o[1]) + o[2]))

    def peer(offset):
        dx, dz, dy = offset
        px = lax.rem(cx + dx, zs // SIDE)
        pz = lax.rem(cz + dz, SIDE)
        return px * SIDE + pz, lax.rem(y + dy, ys)

    loads = []
    for j in range(locals_):
        loads.append(
            (
                pltpu.make_async_copy(wgate_ref.at[0, j], wg.at[j], w_sem.at[3 * j]),
                pltpu.make_async_copy(wup_ref.at[0, j], wu.at[j], w_sem.at[3 * j + 1]),
                pltpu.make_async_copy(wdown_ref.at[0, j], wd.at[j], w_sem.at[3 * j + 2]),
            )
        )

    def from_input(m):
        return pltpu.make_async_copy(hidden_ref.at[m], hbuf.at[m], h_sem.at[m])

    @pl.when(stage == 0)
    def _():
        for m in range(micro):
            from_input(m).start()

    for j in range(locals_):
        loads[j][0].start()
        loads[j][1].start()
    for j in range(locals_):
        loads[j][2].start()

    barrier = pltpu.get_barrier_semaphore()
    for offset in offsets:
        pe, py = peer(offset)
        pl.semaphore_signal(barrier, inc=1, device_id={"exp": pe, "pair": py}, device_id_type=MESH)

    @pl.when(stage > 0)
    def _():
        pl.semaphore_signal(barrier, inc=1, device_id={"pipe": stage - 1}, device_id_type=MESH)

    @pl.when(stage < stages - 1)
    def _():
        pl.semaphore_signal(barrier, inc=1, device_id={"pipe": stage + 1}, device_id_type=MESH)

    def row_parts(index):
        d = fdiv(index, block)
        r = index - block * d
        q = fdiv(r, half)
        t = r - half * q
        j = fdiv(t, SLOTS)
        return d, q, j, t - SLOTS * j

    for u in range(units):
        here = pl.ds(u * unit, unit)
        d, q, j, s = row_parts(iota((unit, LANES), 0) + u * unit)
        lane = iota((unit, LANES), 1)
        sel[here] = jnp.where(lane == locals_ * d + j, 1.0, 0.0).astype(BF16)
        pick_g[here] = jnp.where(fdiv(lane, rows) == q, s + 1.0, -1.0)
        d, q, j, s = row_parts(iota((QUARTERS * rows, unit), 1) + u * unit)
        at = iota((QUARTERS * rows, unit), 0)
        pick_s[:, u * unit : (u + 1) * unit] = jnp.where(fdiv(at, rows) == q, s + 1.0, -1.0)
    d, q, j, s = row_parts(iota((unit, unit), 1))
    spread = (q * locals_ + j) * per + d * SLOTS + s
    unpack[...] = jnp.where(iota((unit, unit), 0) == spread, 1.0, 0.0).astype(BF16)
    d, q, j, s = row_parts(iota((unit, unit), 0))
    spread = (q * locals_ + j) * per + d * SLOTS + s
    repack[...] = jnp.where(iota((unit, unit), 1) == spread, 1.0, 0.0).astype(BF16)

    linked = (stage > 0).astype(jnp.int32) + (stage < stages - 1).astype(jnp.int32)
    pl.semaphore_wait(barrier, len(offsets) + linked)

    def part_of(at):
        return pl.ds(pl.multiple_of(at * block, block), block)

    def out_copy_of(m, c, at, pe, py):
        return pltpu.make_async_remote_copy(
            src_ref=sendbuf.at[m, c, part_of(at)],
            dst_ref=recvbuf.at[m, c, part_of(me)],
            send_sem=a_sem.at[m, c, at],
            recv_sem=ar_sem.at[m, c, me],
            device_id={"exp": pe, "pair": py},
            device_id_type=MESH,
        )

    def in_copy_of(m, c, at, pe, py):
        return pltpu.make_async_remote_copy(
            src_ref=sendbuf.at[m, c, part_of(at)],
            dst_ref=recvbuf.at[m, c, part_of(at)],
            send_sem=a_sem.at[m, c, at],
            recv_sem=ar_sem.at[m, c, at],
            device_id={"exp": pe, "pair": py},
            device_id_type=MESH,
        )

    def back_copy_of(m, c, at, pe, py):
        return pltpu.make_async_remote_copy(
            src_ref=backbuf.at[m, c, part_of(at)],
            dst_ref=homebuf.at[m, c, part_of(me)],
            send_sem=b_sem.at[m, c, at],
            recv_sem=br_sem.at[m, c, me],
            device_id={"exp": pe, "pair": py},
            device_id_type=MESH,
        )

    def home_copy_of(m, c, at, pe, py):
        return pltpu.make_async_remote_copy(
            src_ref=backbuf.at[m, c, part_of(at)],
            dst_ref=homebuf.at[m, c, part_of(at)],
            send_sem=b_sem.at[m, c, at],
            recv_sem=br_sem.at[m, c, at],
            device_id={"exp": pe, "pair": py},
            device_id_type=MESH,
        )

    def hand_copy(m):
        return pltpu.make_async_remote_copy(
            src_ref=obuf.at[m],
            dst_ref=hbuf.at[m],
            send_sem=hs_sem.at[m],
            recv_sem=h_sem.at[m],
            device_id={"pipe": stage + 1},
            device_id_type=MESH,
        )

    def out_copy(m):
        return pltpu.make_async_copy(obuf.at[m], out_ref.at[0, m], o_sem.at[m])

    earlier = (iota((rows, rows), 0) >= iota((rows, rows), 1)).astype(F32).astype(BF16)

    def dispatch(m):
        chosen = routes_ref[0, m]
        probs = probs_ref[0, m]
        normal = probs / jnp.sum(probs, axis=-1, keepdims=True)
        lane = lax.broadcasted_iota(jnp.int32, (rows, LANES), 1)
        mask = jnp.zeros((rows, LANES), F32)
        weight = jnp.zeros((rows, LANES), F32)
        for k in range(chosen.shape[1]):
            hit = lane == chosen[:, k : k + 1]
            mask = mask + jnp.where(hit, 1.0, 0.0)
            weight = weight + jnp.where(hit, normal[:, k : k + 1], 0.0)
        code = (mask * dot(earlier, mask.astype(BF16))).astype(BF16)
        code = jnp.concatenate([code] * QUARTERS, axis=0)
        weight = jnp.concatenate([weight.astype(BF16)] * QUARTERS, axis=0)
        for u in range(units):
            here = pl.ds(u * unit, unit)
            there = slice(u * unit, (u + 1) * unit)
            gath[here] = jnp.where(dot_nt(sel[here], code) == pick_g[here], 1.0, 0.0).astype(BF16)
            hits = dot_nt(code, sel[here]) == pick_s[:, there]
            comb[m, :, there] = jnp.where(hits, dot_nt(weight, sel[here]), 0.0).astype(BF16)

        from_input(m).wait()
        state = hbuf[m].astype(F32)
        scale = lax.rsqrt(jnp.mean(state * state, axis=-1, keepdims=True) + EPS)
        normed = (state * scale * gain_ref[...]).astype(BF16)
        for c in range(CHUNKS):
            for q in range(QUARTERS):
                at = c * cw + q * qw
                xq[q * rows : (q + 1) * rows, c * qw : (c + 1) * qw] = normed[:, at : at + qw]
        for c in range(CHUNKS):
            for u in range(units):
                here = pl.ds(u * unit, unit)
                sendbuf[m, c, here] = dot(gath[here], xq[:, c * qw : (c + 1) * qw]).astype(BF16)
            for offset in offsets:
                pe, py = peer(offset)
                out_copy_of(m, c, pe * ys + py, pe, py).start()
            recvbuf[m, c, part_of(me)] = sendbuf[m, c, part_of(me)]

    def experts(m):
        for c in range(CHUNKS):
            for offset in reversed(offsets):
                pe, py = peer(offset)
                in_copy_of(m, c, pe * ys + py, pe, py).wait_recv()
            for u in range(units):
                apart = dot(unpack[...], recvbuf[m, c, u * unit : (u + 1) * unit]).astype(BF16)
                for q in range(QUARTERS):
                    for j in range(locals_):
                        at = (q * locals_ + j) * per
                        to = c * cw + q * qw
                        xe[j, u * per : (u + 1) * per, to : to + qw] = apart[at : at + per]
            if c == 0:

                @pl.when(m == 0)
                def _():
                    for j in range(locals_):
                        loads[j][0].wait()
                        loads[j][1].wait()

            for j in range(locals_):
                held = xe[j, :, c * cw : (c + 1) * cw]
                for f in range(0, ff, 256):
                    cols = slice(f, f + 256)
                    gate = dot(held, wg[j, c * cw : (c + 1) * cw, cols])
                    upward = dot(held, wu[j, c * cw : (c + 1) * cw, cols])
                    if c > 0:
                        gate = gate + acc[0, j, :, cols]
                        upward = upward + acc[1, j, :, cols]
                    if c < CHUNKS - 1:
                        acc[0, j, :, cols] = gate
                        acc[1, j, :, cols] = upward
                    else:
                        hid[j, :, cols] = (jax.nn.silu(gate) * upward).astype(BF16)

        @pl.when(m == 0)
        def _():
            for j in range(locals_):
                loads[j][2].wait()

        for c in range(CHUNKS):
            for j in range(locals_):
                for q in range(QUARTERS):
                    to = c * cw + q * qw
                    made = dot(hid[j], wd[j, :, to : to + qw]).astype(BF16)
                    at = (q * locals_ + j) * per
                    for u in range(units):
                        stack[u, at : at + per] = made[u * per : (u + 1) * per]
            for u in range(units):
                backbuf[m, c, u * unit : (u + 1) * unit] = dot(repack[...], stack[u]).astype(BF16)
            for offset in offsets:
                pe, py = peer(offset)
                back_copy_of(m, c, pe * ys + py, pe, py).start()
            homebuf[m, c, part_of(me)] = backbuf[m, c, part_of(me)]

    def finish(m):
        for c in range(CHUNKS):
            for offset in reversed(offsets):
                pe, py = peer(offset)
                home_copy_of(m, c, pe * ys + py, pe, py).wait_recv()
            mixed = dot(comb[m], homebuf[m, c])
            for q in range(QUARTERS):
                cols = slice(c * cw + q * qw, c * cw + (q + 1) * qw)
                added = hbuf[m, :, cols].astype(F32) + mixed[q * rows : (q + 1) * rows]
                obuf[m, :, cols] = added.astype(BF16)

        @pl.when(stage < stages - 1)
        def _():
            hand_copy(m).start()

        out_copy(m).start()

    @pl.loop(0, micro + 1)
    def _(i):
        @pl.when(i > 0)
        def _():
            experts(i - 1)

        @pl.when(i < micro)
        def _():
            dispatch(i)

        @pl.when(i > 0)
        def _():
            finish(i - 1)

    @pl.loop(0, micro)
    def _(m):
        for c in range(CHUNKS):
            for offset in offsets:
                pe, py = peer(offset)
                out_copy_of(m, c, pe * ys + py, pe, py).wait_send()
                back_copy_of(m, c, pe * ys + py, pe, py).wait_send()

        @pl.when(stage < stages - 1)
        def _():
            hand_copy(m).wait_send()

        out_copy(m).wait()


def relayed(hidden_in, routes, gate_probs, norm_gain, w_gate, w_up, w_down):
    micro, rows, width = hidden_in.shape
    _, locals_, _, ff = w_gate.shape
    stages, zs, ys = (lax.axis_size(a) for a in ("pipe", "exp", "pair"))
    groups = zs * ys
    block = QUARTERS * locals_ * SLOTS
    total = groups * block
    unit = UNITS * block
    qw = width // CHUNKS // QUARTERS
    dma = pltpu.SemaphoreType.DMA
    anywhere = pl.BlockSpec(memory_space=pl.ANY)
    inside = pl.BlockSpec(memory_space=pltpu.VMEM)
    moved = pltpu.VMEM((micro, CHUNKS, total, qw), BF16)
    return pl.pallas_call(
        functools.partial(relay_kernel, stages, zs, ys),
        out_shape=jax.ShapeDtypeStruct((1, micro, rows, width), BF16),
        in_specs=[anywhere, inside, inside, inside, anywhere, anywhere, anywhere],
        out_specs=anywhere,
        scratch_shapes=[
            pltpu.VMEM((locals_, width, ff), BF16),
            pltpu.VMEM((locals_, width, ff), BF16),
            pltpu.VMEM((locals_, ff, width), BF16),
            pltpu.VMEM((micro, rows, width), BF16),
            pltpu.VMEM((micro, rows, width), BF16),
            pltpu.VMEM((QUARTERS * rows, CHUNKS * qw), BF16),
            moved,
            moved,
            moved,
            moved,
            pltpu.VMEM((locals_, groups * SLOTS, width), BF16),
            pltpu.VMEM((2, locals_, groups * SLOTS, ff), F32),
            pltpu.VMEM((locals_, groups * SLOTS, ff), BF16),
            pltpu.VMEM((groups // UNITS, unit, qw), BF16),
            pltpu.VMEM((total, LANES), BF16),
            pltpu.VMEM((total, LANES), F32),
            pltpu.VMEM((QUARTERS * rows, total), F32),
            pltpu.VMEM((total, LANES), BF16),
            pltpu.VMEM((micro, QUARTERS * rows, total), BF16),
            pltpu.VMEM((unit, unit), BF16),
            pltpu.VMEM((unit, unit), BF16),
            dma((3 * locals_,)),
            dma((micro,)),
            dma((micro,)),
            dma((micro,)),
            dma((micro, CHUNKS, groups)),
            dma((micro, CHUNKS, groups)),
            dma((micro, CHUNKS, groups)),
            dma((micro, CHUNKS, groups)),
        ],
        compiler_params=pltpu.CompilerParams(
            collective_id=0, has_side_effects=True, vmem_limit_bytes=VMEM_LIMIT
        ),
    )(hidden_in, routes, gate_probs, norm_gain, w_gate, w_up, w_down)


def solution(mesh):
    in_specs = (
        P(None, ("exp", "pair"), None),
        P("pipe", None, ("exp", "pair"), None),
        P("pipe", None, ("exp", "pair"), None),
        P("pipe", None),
        P("pipe", ("exp", "pair"), None, None),
        P("pipe", ("exp", "pair"), None, None),
        P("pipe", ("exp", "pair"), None, None),
    )
    out_specs = P("pipe", None, ("exp", "pair"), None)
    return jax.shard_map(
        relayed, mesh=mesh, in_specs=in_specs, out_specs=out_specs, check_vma=False
    )
```

time: 813 us -> 293 us (0.36)
  the two profiles are of different devices: /device:TPU:1 before, /device:TPU:17 now
where the time goes in v1:
time: 293 us
  Pallas kernels  288 us (98%)
  local copies, waits for them, and re-layouts  4.73 us (2%)
    pallas_call x1, Pallas kernels, relayed(): pl.pallas_call(functools.partial(relay_kernel, stages, zs, ys), out_shape...  288 us

profile of v1, /device:TPU:17, one launch (start us, length us, event | category | flops | bytes accessed | tf_op | source)
XLA Modules:
  0.0 292.5 jit_solution(14859023493316420281)
XLA Ops:
  0.0 1.4 copy.8.routes_ref
  1.4 1.4 copy.9.probs_ref
  2.8 287.8 %shard_map.73 = bf16[1,4,32,2048]{3,2,1,0:T(8,128)(2,1)} custom-call(bf16[4,32,2048]{2,1,0:T(8,128)(2,1)} %hidden_ref.1, s32[1,4,32,8]{3,2,1,0:T(8,128)} %copy.8.routes_ref, f32[1,4,32,8]{3,2,1,0:T(8,128)} %copy.9.probs_ref, f32[1,2048]{1,0:T(1,128)} %gain_ref.1, bf16[1,2,2048,768]{3,2,1,0:T(8,128)(2,1)} %wgate_ref.1, bf16[1,2,2048,768]{3,2,1,0:T(8,128)(2,1)} %wup_ref.1, ...), custom_call_target="tpu_custom_call" | custom-call | tf_op jit(solution)/shard_map/pallas_call | solution.py:393
  290.6 1.9 copy.11

commit v2 on v1

v2 whole, which is shorter than its diff:
```python
import functools

import jax
import jax.numpy as jnp
from jax import lax
from jax.experimental import pallas as pl
from jax.experimental.pallas import tpu as pltpu
from jax.sharding import PartitionSpec as P

EPS = 1e-06
MESH = pl.DeviceIdType.MESH
F32 = jnp.float32
BF16 = jnp.bfloat16
VMEM_LIMIT = 63 * 1024 * 1024
SLOTS = 6
SIDE = 4
STRIPS = 8
LANES = 128
UNITS = 8
ORDERED = (False, False, False, False)


def fdiv(value, n):
    return jnp.floor((value + 0.5) * (1.0 / n))


def iota(shape, axis):
    return lax.broadcasted_iota(jnp.int32, shape, axis).astype(F32)


def dot(a, b):
    return jnp.dot(a, b, preferred_element_type=F32)


def dot_nt(a, b):
    return lax.dot_general(a, b, (((1,), (1,)), ((), ())), preferred_element_type=F32)


def relay_kernel(
    stages,
    zs,
    ys,
    hidden_ref,
    routes_ref,
    probs_ref,
    gain_ref,
    wgate_ref,
    wup_ref,
    wdown_ref,
    out_ref,
    wg,
    wu,
    wd,
    hbuf,
    obuf,
    xq,
    sendbuf,
    recvbuf,
    backbuf,
    homebuf,
    xe,
    hid,
    stack,
    sel,
    pick_g,
    pick_s,
    code,
    gath,
    comb,
    unpack,
    repack,
    w_sem,
    h_sem,
    hs_sem,
    o_sem,
    a_sem,
    ar_sem,
    b_sem,
    br_sem,
):
    micro, rows, width = hbuf.shape
    locals_, _, ff = wg.shape
    groups = zs * ys
    block = STRIPS * SLOTS
    qw = width // STRIPS
    unit = UNITS * block
    units = groups // UNITS
    per = UNITS * SLOTS

    stage = lax.axis_index("pipe")
    e_idx = lax.axis_index("exp")
    y = lax.axis_index("pair")
    me = e_idx * ys + y
    cx = lax.div(e_idx, SIDE)
    cz = lax.rem(e_idx, SIDE)

    def ring(d):
        return min(d, SIDE - d)

    offsets = [
        (dx, dz, dy)
        for dx in range(zs // SIDE)
        for dz in range(SIDE)
        for dy in range(ys)
        if dx or dz or dy
    ]
    offsets.sort(key=lambda o: -(ring(o[0]) + ring(o[1]) + o[2]))

    def peer(offset):
        dx, dz, dy = offset
        px = lax.rem(cx + dx, zs // SIDE)
        pz = lax.rem(cz + dz, SIDE)
        return px * SIDE + pz, lax.rem(y + dy, ys)

    loads = []
    for j in range(locals_):
        loads.append(
            (
                pltpu.make_async_copy(wgate_ref.at[0, j], wg.at[j], w_sem.at[3 * j]),
                pltpu.make_async_copy(wup_ref.at[0, j], wu.at[j], w_sem.at[3 * j + 1]),
                pltpu.make_async_copy(wdown_ref.at[0, j], wd.at[j], w_sem.at[3 * j + 2]),
            )
        )

    def from_input(m):
        return pltpu.make_async_copy(hidden_ref.at[m], hbuf.at[m], h_sem.at[m])

    @pl.when(stage == 0)
    def _():
        for m in range(micro):
            from_input(m).start()

    for j in range(locals_):
        for load in loads[j]:
            load.start()

    barrier = pltpu.get_barrier_semaphore()
    for offset in offsets:
        pe, py = peer(offset)
        pl.semaphore_signal(barrier, inc=1, device_id={"exp": pe, "pair": py}, device_id_type=MESH)

    @pl.when(stage > 0)
    def _():
        pl.semaphore_signal(barrier, inc=1, device_id={"pipe": stage - 1}, device_id_type=MESH)

    @pl.when(stage < stages - 1)
    def _():
        pl.semaphore_signal(barrier, inc=1, device_id={"pipe": stage + 1}, device_id_type=MESH)

    def row_parts(index):
        d = fdiv(index, block)
        r = index - block * d
        q = fdiv(r, SLOTS)
        return d, q, r - SLOTS * q

    for u in range(units):
        here = pl.ds(u * unit, unit)
        d, _, _ = row_parts(iota((unit, LANES), 0) + u * unit)
        lane = iota((unit, LANES), 1)
        for j in range(locals_):
            sel[j, here] = jnp.where(lane == locals_ * d + j, 1.0, 0.0).astype(BF16)
        _, q, s = row_parts(iota((unit, STRIPS * rows), 0) + u * unit)
        at = iota((unit, STRIPS * rows), 1)
        pick_g[here] = jnp.where(fdiv(at, rows) == q, s + 1.0, -1.0)
        _, q, s = row_parts(iota((STRIPS * rows, unit), 1) + u * unit)
        at = iota((STRIPS * rows, unit), 0)
        pick_s[:, u * unit : (u + 1) * unit] = jnp.where(fdiv(at, rows) == q, s + 1.0, -1.0)
    d, q, s = row_parts(iota((unit, unit), 1))
    unpack[...] = jnp.where(iota((unit, unit), 0) == q * per + d * SLOTS + s, 1.0, 0.0).astype(BF16)
    d, q, s = row_parts(iota((unit, unit), 0))
    repack[...] = jnp.where(iota((unit, unit), 1) == q * per + d * SLOTS + s, 1.0, 0.0).astype(BF16)

    linked = (stage > 0).astype(jnp.int32) + (stage < stages - 1).astype(jnp.int32)
    pl.semaphore_wait(barrier, len(offsets) + linked)

    def part_of(at):
        return pl.ds(pl.multiple_of(at * block, block), block)

    def out_copy_of(m, c, at, pe, py):
        return pltpu.make_async_remote_copy(
            src_ref=sendbuf.at[m, c, part_of(at)],
            dst_ref=recvbuf.at[m, c, part_of(me)],
            send_sem=a_sem.at[m, c, at],
            recv_sem=ar_sem.at[m, c, me],
            device_id={"exp": pe, "pair": py},
            device_id_type=MESH,
        )

    def in_copy_of(m, c, at, pe, py):
        return pltpu.make_async_remote_copy(
            src_ref=sendbuf.at[m, c, part_of(at)],
            dst_ref=recvbuf.at[m, c, part_of(at)],
            send_sem=a_sem.at[m, c, at],
            recv_sem=ar_sem.at[m, c, at],
            device_id={"exp": pe, "pair": py},
            device_id_type=MESH,
        )

    def back_copy_of(m, c, at, pe, py):
        return pltpu.make_async_remote_copy(
            src_ref=backbuf.at[m, c, part_of(at)],
            dst_ref=homebuf.at[m, c, part_of(me)],
            send_sem=b_sem.at[m, c, at],
            recv_sem=br_sem.at[m, c, me],
            device_id={"exp": pe, "pair": py},
            device_id_type=MESH,
        )

    def home_copy_of(m, c, at, pe, py):
        return pltpu.make_async_remote_copy(
            src_ref=backbuf.at[m, c, part_of(at)],
            dst_ref=homebuf.at[m, c, part_of(at)],
            send_sem=b_sem.at[m, c, at],
            recv_sem=br_sem.at[m, c, at],
            device_id={"exp": pe, "pair": py},
            device_id_type=MESH,
        )

    def hand_copy(m):
        return pltpu.make_async_remote_copy(
            src_ref=obuf.at[m],
            dst_ref=hbuf.at[m],
            send_sem=hs_sem.at[m],
            recv_sem=h_sem.at[m],
            device_id={"pipe": stage + 1},
            device_id_type=MESH,
        )

    def out_copy(m):
        return pltpu.make_async_copy(obuf.at[m], out_ref.at[0, m], o_sem.at[m])

    earlier = (iota((rows, rows), 0) >= iota((rows, rows), 1)).astype(F32).astype(BF16)

    def out_sent(m, j):
        for offset in offsets:
            pe, py = peer(offset)
            out_copy_of(m, j, pe * ys + py, pe, py).wait_send()

    def back_sent(m, j):
        for offset in offsets:
            pe, py = peer(offset)
            back_copy_of(m, j, pe * ys + py, pe, py).wait_send()

    last = locals_ - 1

    def prepare(m):
        chosen = routes_ref[0, m]
        probs = probs_ref[0, m]
        normal = probs / jnp.sum(probs, axis=-1, keepdims=True)
        lane = lax.broadcasted_iota(jnp.int32, (rows, LANES), 1)
        mask = jnp.zeros((rows, LANES), F32)
        weight = jnp.zeros((rows, LANES), F32)
        for k in range(chosen.shape[1]):
            hit = lane == chosen[:, k : k + 1]
            mask = mask + jnp.where(hit, 1.0, 0.0)
            weight = weight + jnp.where(hit, normal[:, k : k + 1], 0.0)
        ranks = (mask * dot(earlier, mask.astype(BF16))).astype(BF16)
        code[...] = jnp.concatenate([ranks] * STRIPS, axis=0)
        weight = jnp.concatenate([weight.astype(BF16)] * STRIPS, axis=0)
        for j in range(locals_):
            for u in range(units):
                here = pl.ds(u * unit, unit)
                there = slice(u * unit, (u + 1) * unit)
                found = dot_nt(sel[j, here], code[...]) == pick_g[here]
                gath[j, here] = jnp.where(found, 1.0, 0.0).astype(BF16)
                hits = dot_nt(code[...], sel[j, here]) == pick_s[:, there]
                shares = jnp.where(hits, dot_nt(weight, sel[j, here]), 0.0)
                comb[lax.rem(m, 2), j, :, there] = shares.astype(BF16)

        from_input(m).wait()
        state = hbuf[m].astype(F32)
        scale = lax.rsqrt(jnp.mean(state * state, axis=-1, keepdims=True) + EPS)
        normed = (state * scale * gain_ref[...]).astype(BF16)
        for q in range(STRIPS):
            xq[q * rows : (q + 1) * rows] = normed[:, q * qw : (q + 1) * qw]

    def dispatch(m, j):
        for u in range(units):
            here = pl.ds(u * unit, unit)
            sendbuf[m, j, here] = dot(gath[j, here], xq[...]).astype(BF16)
        recvbuf[m, j, part_of(me)] = sendbuf[m, j, part_of(me)]
        if j > 0:
            if ORDERED[1]:
                out_sent(m, j - 1)
        elif ORDERED[0]:

            @pl.when(m > 0)
            def _():
                back_sent(m - 1, last)

        for offset in offsets:
            pe, py = peer(offset)
            out_copy_of(m, j, pe * ys + py, pe, py).start()

    def expert(m, j):
        for offset in reversed(offsets):
            pe, py = peer(offset)
            in_copy_of(m, j, pe * ys + py, pe, py).wait_recv()
        for u in range(units):
            apart = dot(unpack[...], recvbuf[m, j, u * unit : (u + 1) * unit]).astype(BF16)
            for q in range(STRIPS):
                xe[u * per : (u + 1) * per, q * qw : (q + 1) * qw] = apart[q * per : (q + 1) * per]

        @pl.when(m == 0)
        def _():
            for load in loads[j]:
                load.wait()

        held = xe[...]
        for f in range(0, ff, 256):
            cols = slice(f, f + 256)
            gate = dot(held, wg[j, :, cols])
            upward = dot(held, wu[j, :, cols])
            hid[:, cols] = (jax.nn.silu(gate) * upward).astype(BF16)
        for q in range(STRIPS):
            made = dot(hid[...], wd[j, :, q * qw : (q + 1) * qw]).astype(BF16)
            for u in range(units):
                stack[u, q * per : (q + 1) * per] = made[u * per : (u + 1) * per]
        for u in range(units):
            backbuf[m, j, u * unit : (u + 1) * unit] = dot(repack[...], stack[u]).astype(BF16)
        homebuf[m, j, part_of(me)] = backbuf[m, j, part_of(me)]
        if j > 0:
            if ORDERED[3]:
                back_sent(m, j - 1)
        elif ORDERED[2]:
            out_sent(m, last)
        for offset in offsets:
            pe, py = peer(offset)
            back_copy_of(m, j, pe * ys + py, pe, py).start()

    def finish(m):
        mixed = jnp.zeros((STRIPS * rows, qw), F32)
        for j in range(locals_):
            for offset in reversed(offsets):
                pe, py = peer(offset)
                home_copy_of(m, j, pe * ys + py, pe, py).wait_recv()
            mixed = mixed + dot(comb[lax.rem(m, 2), j], homebuf[m, j])
        for q in range(STRIPS):
            cols = slice(q * qw, (q + 1) * qw)
            added = hbuf[m, :, cols].astype(F32) + mixed[q * rows : (q + 1) * rows]
            obuf[m, :, cols] = added.astype(BF16)

        @pl.when(stage < stages - 1)
        def _():
            hand_copy(m).start()

        out_copy(m).start()

    @pl.loop(0, micro + 1)
    def _(i):
        @pl.when(i < micro)
        def _():
            prepare(i)
            dispatch(i, 0)

        @pl.when(i > 0)
        def _():
            finish(i - 1)

        @pl.when(i < micro)
        def _():
            for j in range(1, locals_):
                dispatch(i, j)
            for j in range(locals_):
                expert(i, j)

    if ORDERED[0]:
        back_sent(micro - 1, last)

    @pl.loop(0, micro)
    def _(m):
        if not ORDERED[0]:
            back_sent(m, last)
        if not ORDERED[1]:
            for j in range(last):
                out_sent(m, j)
        if not ORDERED[2]:
            out_sent(m, last)
        if not ORDERED[3]:
            for j in range(last):
                back_sent(m, j)

        @pl.when(stage < stages - 1)
        def _():
            hand_copy(m).wait_send()

        out_copy(m).wait()


def relayed(hidden_in, routes, gate_probs, norm_gain, w_gate, w_up, w_down):
    micro, rows, width = hidden_in.shape
    _, locals_, _, ff = w_gate.shape
    stages, zs, ys = (lax.axis_size(a) for a in ("pipe", "exp", "pair"))
    groups = zs * ys
    block = STRIPS * SLOTS
    total = groups * block
    unit = UNITS * block
    qw = width // STRIPS
    spread = STRIPS * rows
    dma = pltpu.SemaphoreType.DMA
    anywhere = pl.BlockSpec(memory_space=pl.ANY)
    inside = pl.BlockSpec(memory_space=pltpu.VMEM)
    moved = pltpu.VMEM((micro, locals_, total, qw), BF16)
    return pl.pallas_call(
        functools.partial(relay_kernel, stages, zs, ys),
        out_shape=jax.ShapeDtypeStruct((1, micro, rows, width), BF16),
        in_specs=[anywhere, inside, inside, inside, anywhere, anywhere, anywhere],
        out_specs=anywhere,
        scratch_shapes=[
            pltpu.VMEM((locals_, width, ff), BF16),
            pltpu.VMEM((locals_, width, ff), BF16),
            pltpu.VMEM((locals_, ff, width), BF16),
            pltpu.VMEM((micro, rows, width), BF16),
            pltpu.VMEM((micro, rows, width), BF16),
            pltpu.VMEM((spread, qw), BF16),
            moved,
            moved,
            moved,
            moved,
            pltpu.VMEM((groups * SLOTS, width), BF16),
            pltpu.VMEM((groups * SLOTS, ff), BF16),
            pltpu.VMEM((groups // UNITS, unit, qw), BF16),
            pltpu.VMEM((locals_, total, LANES), BF16),
            pltpu.VMEM((total, spread), F32),
            pltpu.VMEM((spread, total), F32),
            pltpu.VMEM((spread, LANES), BF16),
            pltpu.VMEM((locals_, total, spread), BF16),
            pltpu.VMEM((2, locals_, spread, total), BF16),
            pltpu.VMEM((unit, unit), BF16),
            pltpu.VMEM((unit, unit), BF16),
            dma((3 * locals_,)),
            dma((micro,)),
            dma((micro,)),
            dma((micro,)),
            dma((micro, locals_, groups)),
            dma((micro, locals_, groups)),
            dma((micro, locals_, groups)),
            dma((micro, locals_, groups)),
        ],
        compiler_params=pltpu.CompilerParams(
            collective_id=0, has_side_effects=True, vmem_limit_bytes=VMEM_LIMIT
        ),
    )(hidden_in, routes, gate_probs, norm_gain, w_gate, w_up, w_down)


def solution(mesh):
    in_specs = (
        P(None, ("exp", "pair"), None),
        P("pipe", None, ("exp", "pair"), None),
        P("pipe", None, ("exp", "pair"), None),
        P("pipe", None),
        P("pipe", ("exp", "pair"), None, None),
        P("pipe", ("exp", "pair"), None, None),
        P("pipe", ("exp", "pair"), None, None),
    )
    out_specs = P("pipe", None, ("exp", "pair"), None)
    return jax.shard_map(
        relayed, mesh=mesh, in_specs=in_specs, out_specs=out_specs, check_vma=False
    )
```

time: 293 us -> 277 us (0.945)
  Pallas kernels: 288 us -> 272 us
    pallas_call x1, Pallas kernels: 288 us -> 272 us  [relayed(): pl.pallas_call(functools.partial(relay_kernel, stages, zs, ys), out_shape...]
where the time goes in v2:
time: 277 us; the launch traced here: 276 us
  Pallas kernels  272 us (98%)
  local copies, waits for them, and re-layouts  4.73 us (2%)
    pallas_call x1, Pallas kernels, relayed(): pl.pallas_call(functools.partial(relay_kernel, stages, zs, ys), out_shape...  272 us

profile of v2, /device:TPU:17, one launch (start us, length us, event | category | flops | bytes accessed | tf_op | source)
XLA Modules:
  0.0 276.5 jit_solution(10888014794686993289)
XLA Ops:
  0.0 1.4 copy.8.routes_ref
  1.4 1.4 copy.9.probs_ref
  2.8 271.8 %shard_map.73 = bf16[1,4,32,2048]{3,2,1,0:T(8,128)(2,1)} custom-call(bf16[4,32,2048]{2,1,0:T(8,128)(2,1)} %hidden_ref.1, s32[1,4,32,8]{3,2,1,0:T(8,128)} %copy.8.routes_ref, f32[1,4,32,8]{3,2,1,0:T(8,128)} %copy.9.probs_ref, f32[1,2048]{1,0:T(1,128)} %gain_ref.1, bf16[1,2,2048,768]{3,2,1,0:T(8,128)(2,1)} %wgate_ref.1, bf16[1,2,2048,768]{3,2,1,0:T(8,128)(2,1)} %wup_ref.1, ...), custom_call_target="tpu_custom_call" | custom-call | tf_op jit(solution)/shard_map/pallas_call | solution.py:404
  274.6 1.9 copy.11

commit v3 on v2

--- a/solution.py
+++ b/solution.py
@@ -17,6 +17,8 @@
 STRIPS = 8
 LANES = 128
 UNITS = 8
+CUTS = 4
+PLACES = ((0, 2, 2), (0, 2, 2), (0, 2, 2), (0, 2, 2))
 ORDERED = (False, False, False, False)
 
 
@@ -41,13 +43,16 @@
     zs,
     ys,
     hidden_ref,
-    routes_ref,
-    probs_ref,
-    gain_ref,
+    routes_hbm,
+    probs_hbm,
+    gain_hbm,
     wgate_ref,
     wup_ref,
     wdown_ref,
     out_ref,
+    routes_ref,
+    probs_ref,
+    gain_ref,
     wg,
     wu,
     wd,
@@ -69,6 +74,7 @@
     comb,
     unpack,
     repack,
+    i_sem,
     w_sem,
     h_sem,
     hs_sem,
@@ -114,16 +120,29 @@
 
     loads = []
     for j in range(locals_):
-        loads.append(
-            (
-                pltpu.make_async_copy(wgate_ref.at[0, j], wg.at[j], w_sem.at[3 * j]),
-                pltpu.make_async_copy(wup_ref.at[0, j], wu.at[j], w_sem.at[3 * j + 1]),
-                pltpu.make_async_copy(wdown_ref.at[0, j], wd.at[j], w_sem.at[3 * j + 2]),
-            )
-        )
+        pieces = []
+        for k, (source, target) in enumerate(
+            ((wgate_ref, wg), (wup_ref, wu), (wdown_ref, wd))
+        ):
+            tall = target.shape[1] // CUTS
+            for cut in range(CUTS):
+                part = pl.ds(cut * tall, tall)
+                sem = w_sem.at[(3 * j + k) * CUTS + cut]
+                pieces.append(
+                    pltpu.make_async_copy(source.at[0, j, part], target.at[j, part], sem)
+                )
+        loads.append(pieces)
 
     def from_input(m):
         return pltpu.make_async_copy(hidden_ref.at[m], hbuf.at[m], h_sem.at[m])
+
+    small = (
+        pltpu.make_async_copy(routes_hbm, routes_ref, i_sem.at[0]),
+        pltpu.make_async_copy(probs_hbm, probs_ref, i_sem.at[1]),
+        pltpu.make_async_copy(gain_hbm, gain_ref, i_sem.at[2]),
+    )
+    for load in small:
+        load.start()
 
     @pl.when(stage == 0)
     def _():
@@ -153,25 +172,16 @@
         q = fdiv(r, SLOTS)
         return d, q, r - SLOTS * q
 
-    for u in range(units):
-        here = pl.ds(u * unit, unit)
-        d, _, _ = row_parts(iota((unit, LANES), 0) + u * unit)
-        lane = iota((unit, LANES), 1)
-        for j in range(locals_):
-            sel[j, here] = jnp.where(lane == locals_ * d + j, 1.0, 0.0).astype(BF16)
-        _, q, s = row_parts(iota((unit, STRIPS * rows), 0) + u * unit)
-        at = iota((unit, STRIPS * rows), 1)
-        pick_g[here] = jnp.where(fdiv(at, rows) == q, s + 1.0, -1.0)
-        _, q, s = row_parts(iota((STRIPS * rows, unit), 1) + u * unit)
-        at = iota((STRIPS * rows, unit), 0)
-        pick_s[:, u * unit : (u + 1) * unit] = jnp.where(fdiv(at, rows) == q, s + 1.0, -1.0)
-    d, q, s = row_parts(iota((unit, unit), 1))
-    unpack[...] = jnp.where(iota((unit, unit), 0) == q * per + d * SLOTS + s, 1.0, 0.0).astype(BF16)
-    d, q, s = row_parts(iota((unit, unit), 0))
-    repack[...] = jnp.where(iota((unit, unit), 1) == q * per + d * SLOTS + s, 1.0, 0.0).astype(BF16)
-
-    linked = (stage > 0).astype(jnp.int32) + (stage < stages - 1).astype(jnp.int32)
-    pl.semaphore_wait(barrier, len(offsets) + linked)
+    down, _, _ = row_parts(iota((unit, 1), 0))
+    lane = iota((unit, LANES), 1)
+    base = lane - locals_ * down
+    for j in range(locals_):
+        for u in range(units):
+            first = locals_ * u * UNITS + j
+            sel[j, pl.ds(u * unit, unit)] = jnp.where(base == first, 1.0, 0.0).astype(BF16)
+    _, q, s = row_parts(iota((unit, 1), 0))
+    pick_g[...] = jnp.where(fdiv(iota((1, STRIPS * rows), 1), rows) == q, s + 1.0, -1.0)
+
 
     def part_of(at):
         return pl.ds(pl.multiple_of(at * block, block), block)
@@ -243,7 +253,17 @@
 
     last = locals_ - 1
 
-    def prepare(m):
+    def settle():
+        _, q, s = row_parts(iota((1, unit), 1))
+        pick_s[...] = jnp.where(fdiv(iota((STRIPS * rows, 1), 0), rows) == q, s + 1.0, -1.0)
+        d, q, s = row_parts(iota((1, unit), 1))
+        moved_to = q * per + d * SLOTS + s
+        unpack[...] = jnp.where(iota((unit, unit), 0) == moved_to, 1.0, 0.0).astype(BF16)
+        d, q, s = row_parts(iota((unit, 1), 0))
+        moved_to = q * per + d * SLOTS + s
+        repack[...] = jnp.where(iota((unit, unit), 1) == moved_to, 1.0, 0.0).astype(BF16)
+
+    def route(m):
         chosen = routes_ref[0, m]
         probs = probs_ref[0, m]
         normal = probs / jnp.sum(probs, axis=-1, keepdims=True)
@@ -255,18 +275,26 @@
             mask = mask + jnp.where(hit, 1.0, 0.0)
             weight = weight + jnp.where(hit, normal[:, k : k + 1], 0.0)
         ranks = (mask * dot(earlier, mask.astype(BF16))).astype(BF16)
-        code[...] = jnp.concatenate([ranks] * STRIPS, axis=0)
-        weight = jnp.concatenate([weight.astype(BF16)] * STRIPS, axis=0)
+        code[0] = jnp.concatenate([ranks] * STRIPS, axis=0)
+        code[1] = jnp.concatenate([weight.astype(BF16)] * STRIPS, axis=0)
+        gather(0)
+
+    def gather(j):
+        for u in range(units):
+            here = pl.ds(u * unit, unit)
+            found = dot_nt(sel[j, here], code[0]) == pick_g[...]
+            gath[j, here] = jnp.where(found, 1.0, 0.0).astype(BF16)
+
+    def weigh(m):
         for j in range(locals_):
             for u in range(units):
                 here = pl.ds(u * unit, unit)
                 there = slice(u * unit, (u + 1) * unit)
-                found = dot_nt(sel[j, here], code[...]) == pick_g[here]
-                gath[j, here] = jnp.where(found, 1.0, 0.0).astype(BF16)
-                hits = dot_nt(code[...], sel[j, here]) == pick_s[:, there]
-                shares = jnp.where(hits, dot_nt(weight, sel[j, here]), 0.0)
+                hits = dot_nt(code[0], sel[j, here]) == pick_s[...]
+                shares = jnp.where(hits, dot_nt(code[1], sel[j, here]), 0.0)
                 comb[lax.rem(m, 2), j, :, there] = shares.astype(BF16)
 
+    def prepare(m):
         from_input(m).wait()
         state = hbuf[m].astype(F32)
         scale = lax.rsqrt(jnp.mean(state * state, axis=-1, keepdims=True) + EPS)
@@ -346,23 +374,63 @@
 
         out_copy(m).start()
 
+    for load in small:
+        load.wait()
+    route(0)
+    linked = (stage > 0).astype(jnp.int32) + (stage < stages - 1).astype(jnp.int32)
+    pl.semaphore_wait(barrier, len(offsets) + linked)
+
     @pl.loop(0, micro + 1)
     def _(i):
+        def finish_at(place):
+            now = i == micro if place == 0 else i < 0
+            for at in range(stages):
+                for step in range(micro - 1):
+                    if PLACES[at][step] == place:
+                        now = jnp.logical_or(now, jnp.logical_and(stage == at, i == step + 1))
+
+            @pl.when(now)
+            def _():
+                finish(i - 1)
+
+        finish_at(0)
+
         @pl.when(i < micro)
         def _():
             prepare(i)
+
+        finish_at(1)
+
+        @pl.when(i < micro)
+        def _():
             dispatch(i, 0)
 
-        @pl.when(i > 0)
-        def _():
-            finish(i - 1)
+        finish_at(2)
 
         @pl.when(i < micro)
         def _():
             for j in range(1, locals_):
+
+                @pl.when(i == 0)
+                def _():
+                    gather(j)
+
                 dispatch(i, j)
+
+        finish_at(3)
+
+        @pl.when(i < micro)
+        def _():
+            pl.when(i == 0)(settle)
+            weigh(i)
             for j in range(locals_):
                 expert(i, j)
+
+        @pl.when(i < micro - 1)
+        def _():
+            route(i + 1)
+            for j in range(1, locals_):
+                gather(j)
 
     if ORDERED[0]:
         back_sent(micro - 1, last)
@@ -399,14 +467,16 @@
     spread = STRIPS * rows
     dma = pltpu.SemaphoreType.DMA
     anywhere = pl.BlockSpec(memory_space=pl.ANY)
-    inside = pl.BlockSpec(memory_space=pltpu.VMEM)
     moved = pltpu.VMEM((micro, locals_, total, qw), BF16)
     return pl.pallas_call(
         functools.partial(relay_kernel, stages, zs, ys),
         out_shape=jax.ShapeDtypeStruct((1, micro, rows, width), BF16),
-        in_specs=[anywhere, inside, inside, inside, anywhere, anywhere, anywhere],
+        in_specs=[anywhere] * 7,
         out_specs=anywhere,
         scratch_shapes=[
+            pltpu.VMEM(routes.shape, jnp.int32),
+            pltpu.VMEM(gate_probs.shape, F32),
+            pltpu.VMEM(norm_gain.shape, F32),
             pltpu.VMEM((locals_, width, ff), BF16),
             pltpu.VMEM((locals_, width, ff), BF16),
             pltpu.VMEM((locals_, ff, width), BF16),
@@ -421,14 +491,15 @@
             pltpu.VMEM((groups * SLOTS, ff), BF16),
             pltpu.VMEM((groups // UNITS, unit, qw), BF16),
             pltpu.VMEM((locals_, total, LANES), BF16),
-            pltpu.VMEM((total, spread), F32),
-            pltpu.VMEM((spread, total), F32),
-            pltpu.VMEM((spread, LANES), BF16),
+            pltpu.VMEM((unit, spread), F32),
+            pltpu.VMEM((spread, unit), F32),
+            pltpu.VMEM((2, spread, LANES), BF16),
             pltpu.VMEM((locals_, total, spread), BF16),
             pltpu.VMEM((2, locals_, spread, total), BF16),
             pltpu.VMEM((unit, unit), BF16),
             pltpu.VMEM((unit, unit), BF16),
-            dma((3 * locals_,)),
+            dma((3,)),
+            dma((3 * locals_ * CUTS,)),
             dma((micro,)),
             dma((micro,)),
             dma((micro,)),

time: 277 us -> 267 us (0.964)
  Pallas kernels: 272 us -> 263 us
    pallas_call x1, Pallas kernels: 272 us -> 263 us  [relayed(): pl.pallas_call(functools.partial(relay_kernel, stages, zs, ys), out_shape...]
where the time goes in v3:
time: 267 us
  Pallas kernels  263 us (99%)
  local copies, waits for them, and re-layouts  4.73 us (2%)
    pallas_call x1, Pallas kernels, relayed(): pl.pallas_call(functools.partial(relay_kernel, stages, zs, ys), out_shape...  263 us

profile of v3, /device:TPU:17, one launch (start us, length us, event | category | flops | bytes accessed | tf_op | source)
XLA Modules:
  0.0 267.2 jit_solution(15567994076839307032)
XLA Ops:
  0.0 1.4 copy.8.routes_hbm
  1.4 1.4 copy.9.probs_hbm
  2.8 262.5 %shard_map.73 = bf16[1,4,32,2048]{3,2,1,0:T(8,128)(2,1)} custom-call(bf16[4,32,2048]{2,1,0:T(8,128)(2,1)} %hidden_ref.1, s32[1,4,32,8]{3,2,1,0:T(8,128)} %copy.8.routes_hbm, f32[1,4,32,8]{3,2,1,0:T(8,128)} %copy.9.probs_hbm, f32[1,2048]{1,0:T(1,128)} %gain_hbm.1, bf16[1,2,2048,768]{3,2,1,0:T(8,128)(2,1)} %wgate_ref.1, bf16[1,2,2048,768]{3,2,1,0:T(8,128)(2,1)} %wup_ref.1, ...), custom_call_target="tpu_custom_call" | custom-call | tf_op jit(solution)/shard_map/pallas_call | solution.py:471
  265.4 1.9 copy.11

commit v4 on v3

--- a/solution.py
+++ b/solution.py
@@ -239,6 +239,7 @@
     def out_copy(m):
         return pltpu.make_async_copy(obuf.at[m], out_ref.at[0, m], o_sem.at[m])
 
+    same = (iota((rows, rows), 0) == iota((rows, rows), 1)).astype(F32).astype(BF16)
     earlier = (iota((rows, rows), 0) >= iota((rows, rows), 1)).astype(F32).astype(BF16)
 
     def out_sent(m, j):
@@ -264,10 +265,10 @@
         repack[...] = jnp.where(iota((unit, unit), 1) == moved_to, 1.0, 0.0).astype(BF16)
 
     def route(m):
-        chosen = routes_ref[0, m]
         probs = probs_ref[0, m]
-        normal = probs / jnp.sum(probs, axis=-1, keepdims=True)
-        lane = lax.broadcasted_iota(jnp.int32, (rows, LANES), 1)
+        normal = dot_nt(same, (probs / jnp.sum(probs, axis=0, keepdims=True)).astype(BF16))
+        chosen = dot_nt(same, routes_ref[0, m].astype(F32).astype(BF16))
+        lane = iota((rows, LANES), 1)
         mask = jnp.zeros((rows, LANES), F32)
         weight = jnp.zeros((rows, LANES), F32)
         for k in range(chosen.shape[1]):
@@ -456,6 +457,8 @@
 
 
 def relayed(hidden_in, routes, gate_probs, norm_gain, w_gate, w_up, w_down):
+    routes = jnp.swapaxes(routes, 2, 3)
+    gate_probs = jnp.swapaxes(gate_probs, 2, 3)
     micro, rows, width = hidden_in.shape
     _, locals_, _, ff = w_gate.shape
     stages, zs, ys = (lax.axis_size(a) for a in ("pipe", "exp", "pair"))

time: 267 us -> 266 us (level)
  local copies, waits for them, and re-layouts: 4.73 us -> 1.88 us
    unnamed x3 -> x1, local copies, waits for them, and re-layouts: 4.73 us -> 1.88 us
where the time goes in v4:
time: 266 us
  Pallas kernels  264 us (99%)
    pallas_call x1, Pallas kernels, relayed(): pl.pallas_call(functools.partial(relay_kernel, stages, zs, ys), out_shape...  264 us

profile of v4, /device:TPU:17, one launch (start us, length us, event | category | flops | bytes accessed | tf_op | source)
XLA Modules:
  0.0 266.0 jit_solution(17037980994275352710)
XLA Ops:
  0.0 264.1 %shard_map.73 = bf16[1,4,32,2048]{3,2,1,0:T(8,128)(2,1)} custom-call(bf16[4,32,2048]{2,1,0:T(8,128)(2,1)} %hidden_ref.1, s32[1,4,8,32]{3,2,1,0:T(8,128)} %bitcast.2, f32[1,4,8,32]{3,2,1,0:T(8,128)} %bitcast.3, f32[1,2048]{1,0:T(1,128)} %gain_hbm.1, bf16[1,2,2048,768]{3,2,1,0:T(8,128)(2,1)} %wgate_ref.1, bf16[1,2,2048,768]{3,2,1,0:T(8,128)(2,1)} %wup_ref.1, ...), custom_call_target="tpu_custom_call" | custom-call | tf_op jit(solution)/shard_map/pallas_call | solution.py:474
  264.1 1.9 copy.9
